TPU v7x, 32 devices: a whole 2x2x4 slice. The times are simulated.
32 devices in a mesh: tok: 16 (over z, x, core), blk: 2 (over y).
Axes of the slice: x: 2, y: 2, z: 4, core: 2. Of those that a mesh axis runs over, the one named last changes fastest.
Arguments:
- activations: bfloat16 [2048, 7168], P('tok', 'blk'), may hold values from -600 to 600
- signs: float32 [7168], P('blk'), may hold values from -1 to 1, as said below
Outputs:
- hessian: float32 [7168, 7168], P('tok', 'blk')
- incoherence: float32 [7168], P('blk')
- largest_ratio: float32 [], replicated
Inputs may be any that keep to these rules, and one draw needn't show every extreme that they name: `signs`: every entry is -1 or 1.
All inputs are finite; a program needn't handle non-finite values.
Results may differ from a plain program's by a relative error of at most 0.0037.
Values may be sent and summed in bfloat16 or wider, within the bound.
No kernel may reach another device: no remote copies, remote signals or barrier semaphores. Data moves between devices by JAX's collectives and lax.ppermute only.
A program may use at most 640 MiB of HBM per device.

v0:
```python
import math
import jax
import jax.numpy as jnp
import numpy as np
from jax import lax
from jax.sharding import PartitionSpec as P

WALSH = 512
MIX = 14
EPS = 1e-06
DAMP = 0.01
LANES = 128


def walsh_np(order):
    index = np.arange(order)
    parity = np.zeros((order, order), np.int64)
    for bit in range(order.bit_length() - 1):
        parity += (index[:, None] >> bit & 1) * (index[None, :] >> bit & 1)
    return (1 - 2 * (parity % 2)).astype(np.float64)


def cosine_np(order):
    k = np.arange(order, dtype=np.float64)[:, None]
    n = np.arange(order, dtype=np.float64)[None, :]
    table = math.sqrt(2.0 / order) * np.cos(math.pi * (n + 0.5) * k / order)
    table[0] *= math.sqrt(0.5)
    return table


def walsh_jnp(order):
    index = jnp.arange(order, dtype=jnp.int32)
    joint = index[:, None] & index[None, :]
    for bit in (16, 8, 4, 2, 1):
        joint = joint ^ joint >> bit
    return (1 - 2 * (joint & 1)).astype(jnp.float32)


def inner_tables(inner):
    cos = (cosine_np(MIX).T / math.sqrt(WALSH)).astype(np.float32)
    high = np.asarray(cos.astype(jnp.bfloat16))
    low = np.asarray((cos - high.astype(np.float32)).astype(jnp.bfloat16))
    walsh = walsh_jnp(inner).astype(jnp.bfloat16)
    tables = []
    for part in (high, low):
        rows = jnp.repeat(jnp.repeat(walsh, MIX, axis=0), MIX, axis=1)
        tables.append(rows * jnp.tile(jnp.asarray(part), (inner, inner)))
    return tables


def pair_route(count, step):
    return [(i, i ^ step) for i in range(count)]


def per_device(activations, signs):
    tokens, width = activations.shape
    blocks = lax.axis_size("blk")
    blk = lax.axis_index("blk")
    groups = lax.axis_size("tok")
    tok = lax.axis_index("tok")
    features = width * blocks
    inner = math.gcd(width // MIX, WALSH // blocks, 64)
    inner_width = inner * MIX
    outer = width // inner_width
    signed = activations * signs.astype(jnp.bfloat16)[None, :]
    tables = inner_tables(inner)

    def spread(part):
        stacked = jnp.concatenate(
            [part[:, i * inner_width : (i + 1) * inner_width] for i in range(outer)], axis=0
        )
        mixed = sum((jnp.dot(stacked, t, preferred_element_type=jnp.float32) for t in tables))
        parts = [mixed[i * tokens : (i + 1) * tokens] for i in range(outer)]
        step = 1
        while step < outer:
            parts = [
                parts[i ^ step] - parts[i] if i & step else parts[i] + parts[i ^ step]
                for i in range(outer)
            ]
            step *= 2
        return jnp.concatenate(parts, axis=1)

    total = None
    for step in range(blocks):
        block = signed if step == 0 else lax.ppermute(signed, "blk", pair_route(blocks, step))
        joint = blk & (blk ^ step)
        parity = sum((joint >> bit & 1 for bit in range(max(1, blocks.bit_length() - 1)))) & 1
        sign = jnp.where(parity == 1, -1.0, 1.0).astype(jnp.float32)
        term = spread(block) * sign
        total = term if total is None else total + term
    rotated = total.astype(jnp.bfloat16)
    wide = rotated.astype(jnp.float32)
    trace_total = jnp.sum(wide * wide, axis=0, keepdims=True).reshape(-1, LANES)
    trace_total = jnp.sum(trace_total, axis=0)
    for axis, count in (("blk", blocks), ("tok", groups)):
        step = 1
        while step < count:
            trace_total += lax.ppermute(trace_total, axis, pair_route(count, step))
            step *= 2
    trace_total = jnp.sum(trace_total)
    diag_mean = trace_total / features + EPS
    all_tokens = lax.all_gather(rotated, "tok", axis=0, tiled=True)
    row_count = features // groups
    owner = tok * row_count // width
    offset = tok * row_count - owner * width
    own_slice = lax.dynamic_slice_in_dim(all_tokens, offset, row_count, 1)
    row_slice = jnp.where(blk == owner, own_slice, 0).astype(jnp.bfloat16)
    for step in range(1, blocks):
        route = []
        for t in range(groups):
            source = t * row_count // width
            route.append((t * blocks + source, t * blocks + (source ^ step)))
        row_slice = row_slice + lax.ppermute(own_slice, ("tok", "blk"), route)
    gram = lax.dot_general(
        row_slice, all_tokens, (((0,), (0,)), ((), ())), preferred_element_type=jnp.float32
    )
    rows = tok * row_count + jnp.arange(row_count, dtype=jnp.int32)[:, None]
    columns = blk * width + jnp.arange(width, dtype=jnp.int32)[None, :]
    on_diag = rows == columns
    row_peak = jnp.max(jnp.where(on_diag, 0.0, jnp.abs(gram)), axis=1)
    hessian = gram / diag_mean + DAMP * on_diag.astype(jnp.float32)
    step = 1
    while step < blocks:
        row_peak = jnp.maximum(row_peak, lax.ppermute(row_peak, "blk", pair_route(blocks, step)))
        step *= 2
    peaks = row_peak[None, :]
    step = 1
    while step < groups:
        other = lax.ppermute(peaks, "tok", pair_route(groups, step))
        upper = tok & step != 0
        peaks = jnp.concatenate(
            [jnp.where(upper, other, peaks), jnp.where(upper, peaks, other)], axis=0
        )
        step *= 2
    peaks = peaks.reshape(features)
    incoherence = lax.dynamic_slice_in_dim(peaks, blk * width, width, 0) / diag_mean
    return (hessian, incoherence, jnp.max(peaks) / diag_mean)


def solution(mesh):
    in_specs = (P("tok", "blk"), P("blk"))
    out_specs = (P("tok", "blk"), P("blk"), P())
    return jax.shard_map(
        per_device, mesh=mesh, in_specs=in_specs, out_specs=out_specs, check_vma=False
    )
```

profile of v0, /device:TPU:0, one launch (start us, length us, event | category | flops | bytes accessed | tf_op | source)
XLA Modules:
  0.0 316.9 jit_solution(6557556047697496267)
XLA Ops:
  7.9 1.2 broadcast_multiply_fusion
  9.2 3.1 collective-permute-start
  13.5 1.4 reshape.35
  14.9 8.8 %tile.8 = bf16[64,14,64,14]{3,2,1,0:T(8,128)(2,1)} broadcast(bf16[14,14]{1,0:T(8,128)(2,1)S(1)} %copy-done.5), dimensions={1,3} | broadcast | bytes 1606024 | tf_op jit(solution)/shard_map/tile | solution.py:47
  23.8 21.6 %tile.9 = bf16[896,896]{1,0:T(8,128)(2,1)S(1)} reshape(bf16[64,14,64,14]{3,2,1,0:T(8,128)(2,1)} %tile.8) | data formatting | bytes 3211264 | tf_op jit(solution)/shard_map/tile | solution.py:47
  45.4 2.3 copy.16
  47.7 4.4 %fusion.13 = f32[512,896]{1,0:T(8,128)} fusion(bf16[896,896]{0,1:T(8,128)(2,1)} %reshape.35, bf16[896,896]{0,1:T(8,128)(2,1)} %copy.16, bf16[128,896]{1,0:T(8,128)(2,1)S(1)} %get-tuple-element.20, bf16[128,896]{1,0:T(8,128)(2,1)S(1)} %get-tuple-element.21, bf16[128,896]{1,0:T(8,128)(2,1)S(1)} %copy-done.3, bf16[128,896]{1,0:T(8,128)(2,1)S(1)} %get-tuple-element.19), kind=kOutput, calls=%fused_computation.22 | convolution fusion | flops 826556416 | bytes 5963776 | tf_op jit(solution)/shard_map/dot_general | solution.py:72
  52.1 8.8 %tile.20 = bf16[64,14,64,14]{3,2,1,0:T(8,128)(2,1)} broadcast(bf16[14,14]{1,0:T(8,128)(2,1)S(1)} %copy-done.4), dimensions={1,3} | broadcast | bytes 1606024 | tf_op jit(solution)/shard_map/tile | solution.py:47
  61.0 21.6 %tile.21 = bf16[896,896]{1,0:T(8,128)(2,1)S(1)} reshape(bf16[64,14,64,14]{3,2,1,0:T(8,128)(2,1)} %tile.20) | data formatting | bytes 3211264 | tf_op jit(solution)/shard_map/tile | solution.py:47
  82.6 2.3 copy.17
  84.9 3.7 %convolution_add_fusion.1 = f32[512,896]{1,0:T(8,128)S(1)} fusion(f32[512,896]{1,0:T(8,128)} %fusion.13, bf16[896,896]{0,1:T(8,128)(2,1)} %reshape.35, bf16[896,896]{0,1:T(8,128)(2,1)} %copy.17, bf16[128,896]{1,0:T(8,128)(2,1)S(1)} %get-tuple-element.20, bf16[128,896]{1,0:T(8,128)(2,1)S(1)} %get-tuple-element.21, bf16[128,896]{1,0:T(8,128)(2,1)S(1)} %copy-done.3, ...), kind=kOutput, calls=%fused_computation.14 | convolution fusion | flops 827015168 | bytes 7798784 | tf_op jit(solution)/shard_map/dot_general | solution.py:72
  88.8 1.5 fusion.37
  91.0 1.3 fusion.9
  92.4 1.3 convolution_add_fusion
  93.8 1.3 multiply_reduce_fusion
  95.1 113.7 %all-gather.2.cloned.1.call-done = bf16[2048,3584]{1,0:T(8,128)(2,1)} async-done(((bf16[128,3584]{1,0:T(8,128)(2,1)}), bf16[2048,3584]{1,0:T(8,128)(2,1)}) %all-gather.2.cloned.1.call-update) | async-done | bytes 14680080 | tf_op jit(solution)/shard_map/all_gather | solution.py:102
  208.9 2.8 constant_dynamic-slice_fusion
  211.7 2.3 copy.18
  214.0 4.6 %collective-permute-start.1 = (bf16[2048,448]{0,1:T(8,128)(2,1)}, bf16[2048,448]{0,1:T(8,128)(2,1)}, u32[]{:S(2)}, u32[]{:S(2)}) collective-permute-start(bf16[2048,448]{0,1:T(8,128)(2,1)} %copy.18), channel_id=1, source_target_pairs={{0,1},{2,3},{4,5},{6,7},{8,9},{10,11},{12,13},{14,15},{17,16},{19,... | collective-permute-start | bytes 5505032 | tf_op jit(solution)/shard_map/ppermute | solution.py:113
  218.7 38.6 %collective-permute-done.2 = f32[128]{0:T(128)S(1)} collective-permute-done((f32[128]{0:T(128)S(1)}, f32[128]{0:T(128)S(1)}, u32[]{:S(2)}, u32[]{:S(2)}) %collective-permute-start.2) | collective-permute-done | bytes 544 | tf_op jit(solution)/shard_map/ppermute | solution.py:98
  259.1 3.0 collective-permute-done.4
  262.2 3.5 %collective-permute-done.5 = f32[128]{0:T(128)S(1)} collective-permute-done((f32[128]{0:T(128)S(1)}, f32[128]{0:T(128)S(1)}, u32[]{:S(2)}, u32[]{:S(2)}) %collective-permute-start.5) | collective-permute-done | bytes 544 | tf_op jit(solution)/shard_map/ppermute | solution.py:98
  265.7 2.5 collective-permute-start.6
  268.2 2.0 collective-permute-done.6
  271.4 3.8 %copy.19 = bf16[2048,448]{1,0:T(8,128)(2,1)} copy(bf16[2048,448]{0,1:T(8,128)(2,1)} %collective-permute-done.1) | data formatting | bytes 3670016 | tf_op jit(solution)/shard_map/ppermute | solution.py:113
  275.2 13.6 %fusion.1 = (f32[448]{0:T(512)S(1)}, f32[448,3584]{1,0:T(8,128)}) fusion(s32[3584]{0:T(1024)S(1)} %iota_add_fusion, s32[448]{0:T(512)S(1)} %iota_add_fusion.1, f32[]{:T(128)S(6)} %add.104, bf16[2048,3584]{1,0:T(8,128)(2,1)} %all-gather.2.cloned.1.call-done, bf16[2048,448]{1,0:T(8,128)(2,1)} %copy.19, bf16[2048,448]{1,0:T(8,128)(2,1)S(1)} %constant_dynamic-slice_fusion, ...), kind=kOutput, calls=%fused_computation.3 | convolution fusion | flops 6589742592 | bytes 24790532 | tf_op jit(solution)/shard_map/dot_general | solution.py:114
  288.8 2.5 collective-permute-start.7
  291.3 1.6 collective-permute-done.7
  294.7 3.0 collective-permute-done.9
  297.9 3.5 %collective-permute-done.10 = f32[4,448]{1,0:T(4,128)S(1)} collective-permute-done((f32[4,448]{1,0:T(4,128)S(1)}, f32[4,448]{1,0:T(4,128)S(1)}, u32[]{:S(2)}, u32[]{:S(2)}) %collective-permute-start.10) | collective-permute-done | bytes 7200 | tf_op jit(solution)/shard_map/ppermute | solution.py:129
  301.5 2.1 collective-permute-start.11
  303.6 2.6 collective-permute-done.11
  (53 shorter events, 9.1 us)
Async XLA Ops:
  7.2 201.7 %all-gather.2.cloned.1.call-start = ((), (), s32[]{:S(2)}) async-start(), calls=%async_computation | async-start | bytes 15597568 | tf_op jit(solution)/shard_map/all_gather | solution.py:102
  9.2 79.6 %collective-permute-start = (bf16[128,3584]{1,0:T(8,128)(2,1)S(1)}, bf16[128,3584]{1,0:T(8,128)(2,1)}, u32[]{:S(2)}, u32[]{:S(2)}) collective-permute-start(bf16[128,3584]{1,0:T(8,128)(2,1)S(1)} %broadcast_multiply_fusion), channel_id=1, source_target_pairs={{0,1},{1,0},{2,3},{3,2},{4,5},{5,4},{6,7},{7,6},{8,9},{9,8},{10,11... | collective-permute-start | bytes 2752520 | tf_op jit(solution)/shard_map/ppermute | solution.py:85
  13.5 1.4 copy-start.5
  45.4 2.4 copy-start.3
  47.7 4.4 %copy-start.4 = (bf16[14,14]{1,0:T(8,128)(2,1)S(1)}, bf16[14,14]{1,0:T(8,128)(2,1)}, u32[]{:S(2)}) copy-start(bf16[14,14]{1,0:T(8,128)(2,1)} %constant.60.clone) | copy-start | bytes 1180
  88.6 1.8 copy-start.2
  88.8 2.2 copy-start.1
  91.0 1.4 copy-start
  214.0 57.4 %collective-permute-start.1 = (bf16[2048,448]{0,1:T(8,128)(2,1)}, bf16[2048,448]{0,1:T(8,128)(2,1)}, u32[]{:S(2)}, u32[]{:S(2)}) collective-permute-start(bf16[2048,448]{0,1:T(8,128)(2,1)} %copy.18), channel_id=1, source_target_pairs={{0,1},{2,3},{4,5},{6,7},{8,9},{10,11},{12,13},{14,15},{17,16},{19,... | collective-permute-start | bytes 5505032 | tf_op jit(solution)/shard_map/ppermute | solution.py:113
  218.6 38.7 %collective-permute-start.2 = (f32[128]{0:T(128)S(1)}, f32[128]{0:T(128)S(1)}, u32[]{:S(2)}, u32[]{:S(2)}) collective-permute-start(f32[128]{0:T(128)S(1)} %bitcast_reduce_fusion), channel_id=1, source_target_pairs={{0,1},{1,0},{2,3},{3,2},{4,5},{5,4},{6,7},{7,6},{8,9},{9,8},{10,11... | collective-permute-start | bytes 1544 | tf_op jit(solution)/shard_map/ppermute | solution.py:98
  257.3 1.2 collective-permute-start.3
  258.5 3.6 %collective-permute-start.4 = (f32[128]{0:T(128)S(1)}, f32[128]{0:T(128)S(1)}, u32[]{:S(2)}, u32[]{:S(2)}) collective-permute-start(f32[128]{0:T(128)S(1)} %add.100), channel_id=1, source_target_pairs={{0,4},{2,6},{4,0},{6,2},{8,12},{10,14},{12,8},{14,10},{16,20},{18,... | collective-permute-start | bytes 1544 | tf_op jit(solution)/shard_map/ppermute | solution.py:98
  262.1 3.6 %collective-permute-start.5 = (f32[128]{0:T(128)S(1)}, f32[128]{0:T(128)S(1)}, u32[]{:S(2)}, u32[]{:S(2)}) collective-permute-start(f32[128]{0:T(128)S(1)} %add.101), channel_id=1, source_target_pairs={{0,8},{2,10},{4,12},{6,14},{8,0},{10,2},{12,4},{14,6},{16,24},{18,... | collective-permute-start | bytes 1544 | tf_op jit(solution)/shard_map/ppermute | solution.py:98
  265.7 4.5 %collective-permute-start.6 = (f32[128]{0:T(128)S(1)}, f32[128]{0:T(128)S(1)}, u32[]{:S(2)}, u32[]{:S(2)}) collective-permute-start(f32[128]{0:T(128)S(1)} %add.102), channel_id=1, source_target_pairs={{0,16},{2,18},{4,20},{6,22},{8,24},{10,26},{12,28},{14,30},{16,0},... | collective-permute-start | bytes 1544 | tf_op jit(solution)/shard_map/ppermute | solution.py:98
  288.8 4.0 %collective-permute-start.7 = (f32[448]{0:T(512)S(1)}, f32[448]{0:T(512)S(1)}, u32[]{:S(2)}, u32[]{:S(2)}) collective-permute-start(f32[448]{0:T(512)S(1)} %get-tuple-element.9), channel_id=1, source_target_pairs={{0,1},{1,0},{2,3},{3,2},{4,5},{5,4},{6,7},{7,6},{8,9},{9,8},{10,11... | collective-permute-start | bytes 5384 | tf_op jit(solution)/shard_map/ppermute | solution.py:124
  292.9 1.2 collective-permute-start.8
  294.1 3.7 %collective-permute-start.9 = (f32[2,448]{1,0:T(2,128)S(1)}, f32[2,448]{1,0:T(2,128)S(1)}, u32[]{:S(2)}, u32[]{:S(2)}) collective-permute-start(f32[2,448]{1,0:T(2,128)S(1)} %pad_maximum_fusion.9), channel_id=1, source_target_pairs={{0,4},{2,6},{4,0},{6,2},{8,12},{10,14},{12,8},{14,10},{16,20},{18,... | collective-permute-start | bytes 10760 | tf_op jit(solution)/shard_map/ppermute | solution.py:129
  297.8 3.7 %collective-permute-start.10 = (f32[4,448]{1,0:T(4,128)S(1)}, f32[4,448]{1,0:T(4,128)S(1)}, u32[]{:S(2)}, u32[]{:S(2)}) collective-permute-start(f32[4,448]{1,0:T(4,128)S(1)} %pad_maximum_fusion.8), channel_id=1, source_target_pairs={{0,8},{2,10},{4,12},{6,14},{8,0},{10,2},{12,4},{14,6},{16,24},{18,... | collective-permute-start | bytes 21512 | tf_op jit(solution)/shard_map/ppermute | solution.py:129
  301.5 4.7 %collective-permute-start.11 = (f32[8,448]{1,0:T(8,128)S(1)}, f32[8,448]{1,0:T(8,128)S(1)}, u32[]{:S(2)}, u32[]{:S(2)}) collective-permute-start(f32[8,448]{1,0:T(8,128)S(1)} %pad_maximum_fusion.7), channel_id=1, source_target_pairs={{0,16},{2,18},{4,20},{6,22},{8,24},{10,26},{12,28},{14,30},{16,0},... | collective-permute-start | bytes 43016 | tf_op jit(solution)/shard_map/ppermute | solution.py:129
Sparse Core Ops, SparseCore 0:
  95.2 113.6 all-gather.1
where the time goes:
time: 317 us
  waiting for transfers between devices  174 us (55%)
  local copies, waits for them, and re-layouts  79.5 us (25%)
  matrix products  24.3 us (8%)
  between operations  17.4 us (5%)
  starting transfers between devices  16.4 us (5%)
  other arithmetic  5.55 us (2%)
    all_gather x1, waiting for transfers between devices, per_device(): all_tokens = lax.all_gather(rotated, 'tok', axis=0, tiled=True)  114 us
    another operation x6, local copies, waits for them, and re-layouts, inner_tables(): tables.append(rows * jnp.tile(jnp.asarray(part), (inner, inner)))  65.6 us
    ppermute x5, waiting for transfers between devices, per_device(): trace_total += lax.ppermute(trace_total, axis, pair_route(count, step))  48.2 us
    dot_general x1, matrix products, per_device(): lax.dot_general(row_slice, all_tokens, (((0,), (0,)), ((), ())), preferre...  13.6 us
    dot_general x4, matrix products, spread(): jnp.dot(stacked, t, preferred_element_type=jnp.float32)  10.6 us
    ppermute x4, waiting for transfers between devices, per_device(): other = lax.ppermute(peaks, 'tok', pair_route(groups, step))  10.3 us
  transfers between devices with their start and end apart: 13, of which 11 were waited for; matrix products, arithmetic and copies ran while one was open for 24% of the time, Pallas kernels for 0%

commit v1 on v0

--- a/solution.py
+++ b/solution.py
@@ -99,7 +99,12 @@
             step *= 2
     trace_total = jnp.sum(trace_total)
     diag_mean = trace_total / features + EPS
-    all_tokens = lax.all_gather(rotated, "tok", axis=0, tiled=True)
+    ring = [rotated]
+    for hop in range(15):
+        ring.append(lax.ppermute(ring[-1], "tok", [(dev, (dev + 1) % 16) for dev in range(16)]))
+    all_tokens = jnp.roll(
+        jnp.concatenate(ring[::-1], axis=0), (lax.axis_index("tok") + 1) * ring[0].shape[0], axis=0
+    )
     row_count = features // groups
     owner = tok * row_count // width
     offset = tok * row_count - owner * width

time: 317 us -> 437 us (1.38)
  waiting for transfers between devices: 174 us -> 286 us
  local copies, waits for them, and re-layouts: 79.5 us -> 108 us
  between operations: 17.4 us -> 4.39 us
  starting transfers between devices: 16.4 us -> 9.07 us
    ppermute x0 -> x15, waiting for transfers between devices: none -> 233 us  [per_device(): lax.ppermute(ring[-1], 'tok', [(dev, (dev + 1) % 16) for dev in range(16)])]
    all_gather x1 -> x0, waiting for transfers between devices: 114 us -> none  [per_device(): all_tokens = lax.all_gather(rotated, 'tok', axis=0, tiled=True)]
    unnamed x12 -> x87, local copies, waits for them, and re-layouts: 0.82 us -> 30.2 us
    ppermute x5, waiting for transfers between devices: 48.2 us -> 38.2 us  [per_device(): trace_total += lax.ppermute(trace_total, axis, pair_route(count, step))]
  transfers between devices with their start and end apart: 13 -> 27, of which waited for: 11 -> 25; matrix products, arithmetic and copies ran while one was open for 24% -> 18% of each run, Pallas kernels for 0% -> 0%
where the time goes in v1:
time: 437 us
  waiting for transfers between devices  286 us (65%)
  local copies, waits for them, and re-layouts  108 us (25%)
  matrix products  24.4 us (6%)
  starting transfers between devices  9.07 us (2%)
  other arithmetic  4.7 us (1%)
  between operations  4.39 us (1%)
    ppermute x15, waiting for transfers between devices, per_device(): lax.ppermute(ring[-1], 'tok', [(dev, (dev + 1) % 16) for dev in range(16)])  233 us
    another operation x6, local copies, waits for them, and re-layouts, inner_tables(): tables.append(rows * jnp.tile(jnp.asarray(part), (inner, inner)))  66.3 us
    ppermute x5, waiting for transfers between devices, per_device(): trace_total += lax.ppermute(trace_total, axis, pair_route(count, step))  38.2 us
    unnamed x87, local copies, waits for them, and re-layouts  30.2 us
    dot_general x1, matrix products, per_device(): lax.dot_general(row_slice, all_tokens, (((0,), (0,)), ((), ())), preferre...  13.6 us
    ppermute x4, waiting for transfers between devices, per_device(): other = lax.ppermute(peaks, 'tok', pair_route(groups, step))  13 us
    dot_general x4, matrix products, spread(): jnp.dot(stacked, t, preferred_element_type=jnp.float32)  10.8 us
  transfers between devices with their start and end apart: 27, of which 25 were waited for; matrix products, arithmetic and copies ran while one was open for 18% of the time, Pallas kernels for 0%

profile of v1, /device:TPU:0, one launch (start us, length us, event | category | flops | bytes accessed | tf_op | source)
XLA Modules:
  0.0 436.8 jit_solution(11940770092766711334)
XLA Ops:
  8.3 9.5 %tile.8 = bf16[64,14,64,14]{3,2,1,0:T(8,128)(2,1)} broadcast(bf16[14,14]{1,0:T(8,128)(2,1)} %constant.93.clone), dimensions={1,3} | broadcast | bytes 1606024 | tf_op jit(solution)/shard_map/tile | solution.py:47
  17.8 21.6 %tile.9 = bf16[896,896]{1,0:T(8,128)(2,1)S(1)} reshape(bf16[64,14,64,14]{3,2,1,0:T(8,128)(2,1)} %tile.8) | data formatting | bytes 3211264 | tf_op jit(solution)/shard_map/tile | solution.py:47
  41.8 4.4 %fusion.14 = f32[512,896]{1,0:T(8,128)} fusion(bf16[896,896]{0,1:T(8,128)(2,1)} %reshape.35, bf16[896,896]{0,1:T(8,128)(2,1)} %copy.16, bf16[128,896]{1,0:T(8,128)(2,1)S(1)} %get-tuple-element.20, bf16[128,896]{1,0:T(8,128)(2,1)S(1)} %get-tuple-element.21, bf16[128,896]{1,0:T(8,128)(2,1)S(1)} %copy-done.26, bf16[128,896]{1,0:T(8,128)(2,1)S(1)} %get-tuple-element.19), kind=kOutput, calls=%fused_computation.23 | convolution fusion | flops 826556416 | bytes 5963776 | tf_op jit(solution)/shard_map/dot_general | solution.py:72
  46.2 8.9 %tile.20 = bf16[64,14,64,14]{3,2,1,0:T(8,128)(2,1)} broadcast(bf16[14,14]{1,0:T(8,128)(2,1)S(1)} %copy-done.27), dimensions={1,3} | broadcast | bytes 1606024 | tf_op jit(solution)/shard_map/tile | solution.py:47
  55.1 21.6 %tile.21 = bf16[896,896]{1,0:T(8,128)(2,1)S(1)} reshape(bf16[64,14,64,14]{3,2,1,0:T(8,128)(2,1)} %tile.20) | data formatting | bytes 3211264 | tf_op jit(solution)/shard_map/tile | solution.py:47
  79.1 3.9 convolution_add_fusion.1
  87.8 15.5 %collective-permute-done.1 = bf16[128,3584]{1,0:T(8,128)(2,1)S(1)} collective-permute-done((bf16[128,3584]{1,0:T(8,128)(2,1)S(1)}, bf16[128,3584]{1,0:T(8,128)(2,1)S(1)}, u32[]{:S(2)}, u32[]{:S(2)}) %collective-permute-start.1) | collective-permute-done | bytes 917536 | tf_op jit(solution)/shard_map/ppermute | solution.py:104
  103.3 15.5 %collective-permute-done.2 = bf16[128,3584]{1,0:T(8,128)(2,1)S(1)} collective-permute-done((bf16[128,3584]{1,0:T(8,128)(2,1)S(1)}, bf16[128,3584]{1,0:T(8,128)(2,1)S(1)}, u32[]{:S(2)}, u32[]{:S(2)}) %collective-permute-start.2) | collective-permute-done | bytes 917536 | tf_op jit(solution)/shard_map/ppermute | solution.py:104
  118.8 15.5 %collective-permute-done.3 = bf16[128,3584]{1,0:T(8,128)(2,1)S(1)} collective-permute-done((bf16[128,3584]{1,0:T(8,128)(2,1)S(1)}, bf16[128,3584]{1,0:T(8,128)(2,1)S(1)}, u32[]{:S(2)}, u32[]{:S(2)}) %collective-permute-start.3) | collective-permute-done | bytes 917536 | tf_op jit(solution)/shard_map/ppermute | solution.py:104
  135.3 15.5 %collective-permute-done.4 = bf16[128,3584]{1,0:T(8,128)(2,1)S(1)} collective-permute-done((bf16[128,3584]{1,0:T(8,128)(2,1)S(1)}, bf16[128,3584]{1,0:T(8,128)(2,1)S(1)}, u32[]{:S(2)}, u32[]{:S(2)}) %collective-permute-start.4) | collective-permute-done | bytes 917536 | tf_op jit(solution)/shard_map/ppermute | solution.py:104
  151.7 15.5 %collective-permute-done.5 = bf16[128,3584]{1,0:T(8,128)(2,1)S(1)} collective-permute-done((bf16[128,3584]{1,0:T(8,128)(2,1)S(1)}, bf16[128,3584]{1,0:T(8,128)(2,1)S(1)}, u32[]{:S(2)}, u32[]{:S(2)}) %collective-permute-start.5) | collective-permute-done | bytes 917536 | tf_op jit(solution)/shard_map/ppermute | solution.py:104
  168.2 15.5 %collective-permute-done.6 = bf16[128,3584]{1,0:T(8,128)(2,1)S(1)} collective-permute-done((bf16[128,3584]{1,0:T(8,128)(2,1)S(1)}, bf16[128,3584]{1,0:T(8,128)(2,1)S(1)}, u32[]{:S(2)}, u32[]{:S(2)}) %collective-permute-start.6) | collective-permute-done | bytes 917536 | tf_op jit(solution)/shard_map/ppermute | solution.py:104
  184.6 15.5 %collective-permute-done.7 = bf16[128,3584]{1,0:T(8,128)(2,1)S(1)} collective-permute-done((bf16[128,3584]{1,0:T(8,128)(2,1)S(1)}, bf16[128,3584]{1,0:T(8,128)(2,1)S(1)}, u32[]{:S(2)}, u32[]{:S(2)}) %collective-permute-start.7) | collective-permute-done | bytes 917536 | tf_op jit(solution)/shard_map/ppermute | solution.py:104
  201.1 15.5 %collective-permute-done.8 = bf16[128,3584]{1,0:T(8,128)(2,1)S(1)} collective-permute-done((bf16[128,3584]{1,0:T(8,128)(2,1)S(1)}, bf16[128,3584]{1,0:T(8,128)(2,1)S(1)}, u32[]{:S(2)}, u32[]{:S(2)}) %collective-permute-start.8) | collective-permute-done | bytes 917536 | tf_op jit(solution)/shard_map/ppermute | solution.py:104
  217.6 15.5 %collective-permute-done.9 = bf16[128,3584]{1,0:T(8,128)(2,1)S(1)} collective-permute-done((bf16[128,3584]{1,0:T(8,128)(2,1)S(1)}, bf16[128,3584]{1,0:T(8,128)(2,1)S(1)}, u32[]{:S(2)}, u32[]{:S(2)}) %collective-permute-start.9) | collective-permute-done | bytes 917536 | tf_op jit(solution)/shard_map/ppermute | solution.py:104
  234.1 15.5 %collective-permute-done.10 = bf16[128,3584]{1,0:T(8,128)(2,1)S(1)} collective-permute-done((bf16[128,3584]{1,0:T(8,128)(2,1)S(1)}, bf16[128,3584]{1,0:T(8,128)(2,1)S(1)}, u32[]{:S(2)}, u32[]{:S(2)}) %collective-permute-start.10) | collective-permute-done | bytes 917536 | tf_op jit(solution)/shard_map/ppermute | solution.py:104
  250.5 15.5 %collective-permute-done.11 = bf16[128,3584]{1,0:T(8,128)(2,1)S(1)} collective-permute-done((bf16[128,3584]{1,0:T(8,128)(2,1)S(1)}, bf16[128,3584]{1,0:T(8,128)(2,1)S(1)}, u32[]{:S(2)}, u32[]{:S(2)}) %collective-permute-start.11) | collective-permute-done | bytes 917536 | tf_op jit(solution)/shard_map/ppermute | solution.py:104
  267.0 15.5 %collective-permute-done.12 = bf16[128,3584]{1,0:T(8,128)(2,1)S(1)} collective-permute-done((bf16[128,3584]{1,0:T(8,128)(2,1)S(1)}, bf16[128,3584]{1,0:T(8,128)(2,1)S(1)}, u32[]{:S(2)}, u32[]{:S(2)}) %collective-permute-start.12) | collective-permute-done | bytes 917536 | tf_op jit(solution)/shard_map/ppermute | solution.py:104
  283.4 15.5 %collective-permute-done.13 = bf16[128,3584]{1,0:T(8,128)(2,1)S(1)} collective-permute-done((bf16[128,3584]{1,0:T(8,128)(2,1)S(1)}, bf16[128,3584]{1,0:T(8,128)(2,1)S(1)}, u32[]{:S(2)}, u32[]{:S(2)}) %collective-permute-start.13) | collective-permute-done | bytes 917536 | tf_op jit(solution)/shard_map/ppermute | solution.py:104
  299.9 15.6 %collective-permute-done.14 = bf16[128,3584]{1,0:T(8,128)(2,1)} collective-permute-done((bf16[128,3584]{1,0:T(8,128)(2,1)S(1)}, bf16[128,3584]{1,0:T(8,128)(2,1)}, u32[]{:S(2)}, u32[]{:S(2)}) %collective-permute-start.14) | collective-permute-done | bytes 917536 | tf_op jit(solution)/shard_map/ppermute | solution.py:104
  315.5 15.8 %collective-permute-done.15 = bf16[128,3584]{1,0:T(8,128)(2,1)} collective-permute-done((bf16[128,3584]{1,0:T(8,128)(2,1)}, bf16[128,3584]{1,0:T(8,128)(2,1)}, u32[]{:S(2)}, u32[]{:S(2)}) %collective-permute-start.15) | collective-permute-done | bytes 917536 | tf_op jit(solution)/shard_map/ppermute | solution.py:104
  341.9 9.7 %copy-done.25 = bf16[4096,3584]{1,0:T(8,128)(2,1)} copy-done((bf16[4096,3584]{1,0:T(8,128)(2,1)}, bf16[4096,3584]{1,0:T(8,128)(2,1)S(1)}, u32[]{:S(2)}) %copy-start.25) | copy-done | bytes 29360152
  355.2 3.2 collective-permute-start.16
  358.4 25.4 %collective-permute-done.17 = f32[128]{0:T(128)S(1)} collective-permute-done((f32[128]{0:T(128)S(1)}, f32[128]{0:T(128)S(1)}, u32[]{:S(2)}, u32[]{:S(2)}) %collective-permute-start.17) | collective-permute-done | bytes 544 | tf_op jit(solution)/shard_map/ppermute | solution.py:98
  385.0 3.6 collective-permute-done.19
  388.6 3.6 collective-permute-done.20
  392.2 4.5 %collective-permute-done.21 = f32[128]{0:T(128)S(1)} collective-permute-done((f32[128]{0:T(128)S(1)}, f32[128]{0:T(128)S(1)}, u32[]{:S(2)}, u32[]{:S(2)}) %collective-permute-start.21) | collective-permute-done | bytes 544 | tf_op jit(solution)/shard_map/ppermute | solution.py:98
  397.9 4.0 copy.19
  401.9 13.6 %fusion.3 = (f32[448]{0:T(512)S(1)}, f32[448,3584]{1,0:T(8,128)}) fusion(s32[3584]{0:T(1024)S(1)} %iota_add_fusion, s32[448]{0:T(512)S(1)} %iota_add_fusion.1, f32[]{:T(128)S(6)} %add.122, bf16[4096,3584]{1,0:T(8,128)(2,1)} %copy-done.25, s32[]{:T(128)S(6)} %select_n.99, bf16[2048,448]{1,0:T(8,128)(2,1)} %copy.19, bf16[2048,448]{1,0:T(8,128)(2,1)S(1)} %dynamic_slice.10, ...), kind=kOutput, calls=%fused_computation.5 | convolution fusion | flops 6589742592 | bytes 25052680 | tf_op jit(solution)/shard_map/dot_general | solution.py:119
  420.9 3.6 collective-permute-done.24
  424.6 3.6 collective-permute-done.25
  428.3 4.6 %collective-permute-done.26 = f32[8,448]{1,0:T(8,128)S(1)} collective-permute-done((f32[8,448]{1,0:T(8,128)S(1)}, f32[8,448]{1,0:T(8,128)S(1)}, u32[]{:S(2)}, u32[]{:S(2)}) %collective-permute-start.26) | collective-permute-done | bytes 14368 | tf_op jit(solution)/shard_map/ppermute | solution.py:134
  (156 shorter events, 50.1 us)
Async XLA Ops:
  2.6 80.5 %collective-permute-start = (bf16[128,3584]{1,0:T(8,128)(2,1)S(1)}, bf16[128,3584]{1,0:T(8,128)(2,1)}, u32[]{:S(2)}, u32[]{:S(2)}) collective-permute-start(bf16[128,3584]{1,0:T(8,128)(2,1)S(1)} %broadcast_multiply_fusion), channel_id=1, source_target_pairs={{0,1},{1,0},{2,3},{3,2},{4,5},{5,4},{6,7},{7,6},{8,9},{9,8},{10,11... | collective-permute-start | bytes 2752520 | tf_op jit(solution)/shard_map/ppermute | solution.py:85
  17.8 24.0 %copy-start.26 = (bf16[128,896]{1,0:T(8,128)(2,1)S(1)}, bf16[128,896]{1,0:T(8,128)(2,1)}, u32[]{:S(2)}) copy-start(bf16[128,896]{1,0:T(8,128)(2,1)} %get-tuple-element.22) | copy-start | bytes 688132
  87.7 15.6 %collective-permute-start.1 = (bf16[128,3584]{1,0:T(8,128)(2,1)S(1)}, bf16[128,3584]{1,0:T(8,128)(2,1)S(1)}, u32[]{:S(2)}, u32[]{:S(2)}) collective-permute-start(bf16[128,3584]{1,0:T(8,128)(2,1)S(1)} %get-tuple-element.8), channel_id=1, source_target_pairs={{0,2},{2,4},{4,6},{6,8},{8,10},{10,12},{12,14},{14,16},{16,18},{18... | collective-permute-start | bytes 2752520 | tf_op jit(solution)/shard_map/ppermute | solution.py:104
  103.3 15.5 %collective-permute-start.2 = (bf16[128,3584]{1,0:T(8,128)(2,1)S(1)}, bf16[128,3584]{1,0:T(8,128)(2,1)S(1)}, u32[]{:S(2)}, u32[]{:S(2)}) collective-permute-start(bf16[128,3584]{1,0:T(8,128)(2,1)S(1)} %collective-permute-done.1), channel_id=1, source_target_pairs={{0,2},{2,4},{4,6},{6,8},{8,10},{10,12},{12,14},{14,16},{16,18},{18... | collective-permute-start | bytes 2752520 | tf_op jit(solution)/shard_map/ppermute | solution.py:104
  118.8 15.5 %collective-permute-start.3 = (bf16[128,3584]{1,0:T(8,128)(2,1)S(1)}, bf16[128,3584]{1,0:T(8,128)(2,1)S(1)}, u32[]{:S(2)}, u32[]{:S(2)}) collective-permute-start(bf16[128,3584]{1,0:T(8,128)(2,1)S(1)} %collective-permute-done.2), channel_id=1, source_target_pairs={{0,2},{2,4},{4,6},{6,8},{8,10},{10,12},{12,14},{14,16},{16,18},{18... | collective-permute-start | bytes 2752520 | tf_op jit(solution)/shard_map/ppermute | solution.py:104
  135.3 15.5 %collective-permute-start.4 = (bf16[128,3584]{1,0:T(8,128)(2,1)S(1)}, bf16[128,3584]{1,0:T(8,128)(2,1)S(1)}, u32[]{:S(2)}, u32[]{:S(2)}) collective-permute-start(bf16[128,3584]{1,0:T(8,128)(2,1)S(1)} %collective-permute-done.3), channel_id=1, source_target_pairs={{0,2},{2,4},{4,6},{6,8},{8,10},{10,12},{12,14},{14,16},{16,18},{18... | collective-permute-start | bytes 2752520 | tf_op jit(solution)/shard_map/ppermute | solution.py:104
  151.7 15.5 %collective-permute-start.5 = (bf16[128,3584]{1,0:T(8,128)(2,1)S(1)}, bf16[128,3584]{1,0:T(8,128)(2,1)S(1)}, u32[]{:S(2)}, u32[]{:S(2)}) collective-permute-start(bf16[128,3584]{1,0:T(8,128)(2,1)S(1)} %collective-permute-done.4), channel_id=1, source_target_pairs={{0,2},{2,4},{4,6},{6,8},{8,10},{10,12},{12,14},{14,16},{16,18},{18... | collective-permute-start | bytes 2752520 | tf_op jit(solution)/shard_map/ppermute | solution.py:104
  168.2 15.5 %collective-permute-start.6 = (bf16[128,3584]{1,0:T(8,128)(2,1)S(1)}, bf16[128,3584]{1,0:T(8,128)(2,1)S(1)}, u32[]{:S(2)}, u32[]{:S(2)}) collective-permute-start(bf16[128,3584]{1,0:T(8,128)(2,1)S(1)} %collective-permute-done.5), channel_id=1, source_target_pairs={{0,2},{2,4},{4,6},{6,8},{8,10},{10,12},{12,14},{14,16},{16,18},{18... | collective-permute-start | bytes 2752520 | tf_op jit(solution)/shard_map/ppermute | solution.py:104
  184.6 15.5 %collective-permute-start.7 = (bf16[128,3584]{1,0:T(8,128)(2,1)S(1)}, bf16[128,3584]{1,0:T(8,128)(2,1)S(1)}, u32[]{:S(2)}, u32[]{:S(2)}) collective-permute-start(bf16[128,3584]{1,0:T(8,128)(2,1)S(1)} %collective-permute-done.6), channel_id=1, source_target_pairs={{0,2},{2,4},{4,6},{6,8},{8,10},{10,12},{12,14},{14,16},{16,18},{18... | collective-permute-start | bytes 2752520 | tf_op jit(solution)/shard_map/ppermute | solution.py:104
  201.1 15.5 %collective-permute-start.8 = (bf16[128,3584]{1,0:T(8,128)(2,1)S(1)}, bf16[128,3584]{1,0:T(8,128)(2,1)S(1)}, u32[]{:S(2)}, u32[]{:S(2)}) collective-permute-start(bf16[128,3584]{1,0:T(8,128)(2,1)S(1)} %collective-permute-done.7), channel_id=1, source_target_pairs={{0,2},{2,4},{4,6},{6,8},{8,10},{10,12},{12,14},{14,16},{16,18},{18... | collective-permute-start | bytes 2752520 | tf_op jit(solution)/shard_map/ppermute | solution.py:104
  217.6 15.5 %collective-permute-start.9 = (bf16[128,3584]{1,0:T(8,128)(2,1)S(1)}, bf16[128,3584]{1,0:T(8,128)(2,1)S(1)}, u32[]{:S(2)}, u32[]{:S(2)}) collective-permute-start(bf16[128,3584]{1,0:T(8,128)(2,1)S(1)} %collective-permute-done.8), channel_id=1, source_target_pairs={{0,2},{2,4},{4,6},{6,8},{8,10},{10,12},{12,14},{14,16},{16,18},{18... | collective-permute-start | bytes 2752520 | tf_op jit(solution)/shard_map/ppermute | solution.py:104
  234.1 15.5 %collective-permute-start.10 = (bf16[128,3584]{1,0:T(8,128)(2,1)S(1)}, bf16[128,3584]{1,0:T(8,128)(2,1)S(1)}, u32[]{:S(2)}, u32[]{:S(2)}) collective-permute-start(bf16[128,3584]{1,0:T(8,128)(2,1)S(1)} %collective-permute-done.9), channel_id=1, source_target_pairs={{0,2},{2,4},{4,6},{6,8},{8,10},{10,12},{12,14},{14,16},{16,18},{18... | collective-permute-start | bytes 2752520 | tf_op jit(solution)/shard_map/ppermute | solution.py:104
  250.5 15.5 %collective-permute-start.11 = (bf16[128,3584]{1,0:T(8,128)(2,1)S(1)}, bf16[128,3584]{1,0:T(8,128)(2,1)S(1)}, u32[]{:S(2)}, u32[]{:S(2)}) collective-permute-start(bf16[128,3584]{1,0:T(8,128)(2,1)S(1)} %collective-permute-done.10), channel_id=1, source_target_pairs={{0,2},{2,4},{4,6},{6,8},{8,10},{10,12},{12,14},{14,16},{16,18},{18... | collective-permute-start | bytes 2752520 | tf_op jit(solution)/shard_map/ppermute | solution.py:104
  267.0 15.5 %collective-permute-start.12 = (bf16[128,3584]{1,0:T(8,128)(2,1)S(1)}, bf16[128,3584]{1,0:T(8,128)(2,1)S(1)}, u32[]{:S(2)}, u32[]{:S(2)}) collective-permute-start(bf16[128,3584]{1,0:T(8,128)(2,1)S(1)} %collective-permute-done.11), channel_id=1, source_target_pairs={{0,2},{2,4},{4,6},{6,8},{8,10},{10,12},{12,14},{14,16},{16,18},{18... | collective-permute-start | bytes 2752520 | tf_op jit(solution)/shard_map/ppermute | solution.py:104
  283.4 15.5 %collective-permute-start.13 = (bf16[128,3584]{1,0:T(8,128)(2,1)S(1)}, bf16[128,3584]{1,0:T(8,128)(2,1)S(1)}, u32[]{:S(2)}, u32[]{:S(2)}) collective-permute-start(bf16[128,3584]{1,0:T(8,128)(2,1)S(1)} %collective-permute-done.12), channel_id=1, source_target_pairs={{0,2},{2,4},{4,6},{6,8},{8,10},{10,12},{12,14},{14,16},{16,18},{18... | collective-permute-start | bytes 2752520 | tf_op jit(solution)/shard_map/ppermute | solution.py:104
  299.9 15.6 %collective-permute-start.14 = (bf16[128,3584]{1,0:T(8,128)(2,1)S(1)}, bf16[128,3584]{1,0:T(8,128)(2,1)}, u32[]{:S(2)}, u32[]{:S(2)}) collective-permute-start(bf16[128,3584]{1,0:T(8,128)(2,1)S(1)} %collective-permute-done.13), channel_id=1, source_target_pairs={{0,2},{2,4},{4,6},{6,8},{8,10},{10,12},{12,14},{14,16},{16,18},{18... | collective-permute-start | bytes 2752520 | tf_op jit(solution)/shard_map/ppermute | solution.py:104
  315.5 15.8 %collective-permute-start.15 = (bf16[128,3584]{1,0:T(8,128)(2,1)}, bf16[128,3584]{1,0:T(8,128)(2,1)}, u32[]{:S(2)}, u32[]{:S(2)}) collective-permute-start(bf16[128,3584]{1,0:T(8,128)(2,1)} %collective-permute-done.14), channel_id=1, source_target_pairs={{0,2},{2,4},{4,6},{6,8},{8,10},{10,12},{12,14},{14,16},{16,18},{18... | collective-permute-start | bytes 2752520 | tf_op jit(solution)/shard_map/ppermute | solution.py:104
  315.5 21.1 %copy-start.17 = (bf16[128,3584]{1,0:T(8,128)(2,1)S(1)}, bf16[128,3584]{1,0:T(8,128)(2,1)}, u32[]{:S(2)}) copy-start(bf16[128,3584]{1,0:T(8,128)(2,1)} %copy-done.16) | copy-start | bytes 2752516
  315.5 21.2 %copy-start.15 = (bf16[128,3584]{1,0:T(8,128)(2,1)S(1)}, bf16[128,3584]{1,0:T(8,128)(2,1)}, u32[]{:S(2)}) copy-start(bf16[128,3584]{1,0:T(8,128)(2,1)} %copy-done.14) | copy-start | bytes 2752516
  315.5 21.2 %copy-start.13 = (bf16[128,3584]{1,0:T(8,128)(2,1)S(1)}, bf16[128,3584]{1,0:T(8,128)(2,1)}, u32[]{:S(2)}) copy-start(bf16[128,3584]{1,0:T(8,128)(2,1)} %copy-done.12) | copy-start | bytes 2752516
  315.5 21.3 %copy-start.11 = (bf16[128,3584]{1,0:T(8,128)(2,1)S(1)}, bf16[128,3584]{1,0:T(8,128)(2,1)}, u32[]{:S(2)}) copy-start(bf16[128,3584]{1,0:T(8,128)(2,1)} %copy-done.10) | copy-start | bytes 2752516
  355.2 42.7 %collective-permute-start.16 = (bf16[2048,448]{0,1:T(8,128)(2,1)}, bf16[2048,448]{0,1:T(8,128)(2,1)}, u32[]{:S(2)}, u32[]{:S(2)}) collective-permute-start(bf16[2048,448]{0,1:T(8,128)(2,1)} %copy.18), channel_id=1, source_target_pairs={{0,1},{2,3},{4,5},{6,7},{8,9},{10,11},{12,13},{14,15},{17,16},{19,... | collective-permute-start | bytes 5505032 | tf_op jit(solution)/shard_map/ppermute | solution.py:118
  358.3 25.5 %collective-permute-start.17 = (f32[128]{0:T(128)S(1)}, f32[128]{0:T(128)S(1)}, u32[]{:S(2)}, u32[]{:S(2)}) collective-permute-start(f32[128]{0:T(128)S(1)} %bitcast_reduce_fusion), channel_id=1, source_target_pairs={{0,1},{1,0},{2,3},{3,2},{4,5},{5,4},{6,7},{7,6},{8,9},{9,8},{10,11... | collective-permute-start | bytes 1544 | tf_op jit(solution)/shard_map/ppermute | solution.py:98
  383.8 1.2 collective-permute-start.18
  385.0 3.6 collective-permute-start.19
  388.6 3.6 collective-permute-start.20
  392.1 4.5 %collective-permute-start.21 = (f32[128]{0:T(128)S(1)}, f32[128]{0:T(128)S(1)}, u32[]{:S(2)}, u32[]{:S(2)}) collective-permute-start(f32[128]{0:T(128)S(1)} %add.120), channel_id=1, source_target_pairs={{0,16},{2,18},{4,20},{6,22},{8,24},{10,26},{12,28},{14,30},{16,0},... | collective-permute-start | bytes 1544 | tf_op jit(solution)/shard_map/ppermute | solution.py:98
  415.6 4.0 collective-permute-start.22
  419.6 1.2 collective-permute-start.23
  420.8 3.7 collective-permute-start.24
  424.5 3.7 collective-permute-start.25
  428.2 4.7 %collective-permute-start.26 = (f32[8,448]{1,0:T(8,128)S(1)}, f32[8,448]{1,0:T(8,128)S(1)}, u32[]{:S(2)}, u32[]{:S(2)}) collective-permute-start(f32[8,448]{1,0:T(8,128)S(1)} %pad_maximum_fusion.7), channel_id=1, source_target_pairs={{0,16},{2,18},{4,20},{6,22},{8,24},{10,26},{12,28},{14,30},{16,0},... | collective-permute-start | bytes 43016 | tf_op jit(solution)/shard_map/ppermute | solution.py:134
  (23 other events, 58.5 us)
